TPU v7x, 32 devices: a whole 2x2x4 slice. The times are simulated.
32 devices in a mesh: ga: 2 (over x), ta: 4 (over y, core), gy: 4 (over z).
Axes of the slice: x: 2, y: 2, z: 4, core: 2. Of those that a mesh axis runs over, the one named last changes fastest.
Arguments:
- clip: bfloat16 [32, 16, 64, 512], P(('ga', 'ta'), 'gy'), parts along dimension 0, may hold values from -6 to 6
- w_space: bfloat16 [3, 3, 512, 512], replicated, may hold values from -0.09375 to 0.09375
- w_time: bfloat16 [3, 512, 512], replicated, may hold values from -0.15625 to 0.15625
- w_qkv: bfloat16 [512, 1536], replicated, may hold values from -0.61871843 to 0.61871843
- w_out: bfloat16 [512, 512], replicated, may hold values from -0.25 to 0.25
- norm_gain: float32 [512], replicated, may hold values from 0.1 to 1.9
Outputs:
- block_out: bfloat16 [32, 16, 64, 512], P(('ga', 'ta'), 'gy'), parts along dimension 0
There are 2 independent parts, one for each index of `ga`. A program takes and returns all parts, laid end to end along the dimension named above; an argument that names none is the same for every part. Nothing has to cross between parts.
All inputs are finite; a program needn't handle non-finite values.
Results may differ from a plain program's by a relative error of at most 0.0085.
Values may be sent and summed in bfloat16 or wider, within the bound.
No kernel may reach another device: no remote copies, remote signals or barrier semaphores. Data moves between devices by JAX's collectives and lax.ppermute only.
A program may use at most 64 MiB of HBM per device.

v0:
```python
import jax
import jax.numpy as jnp
from jax import lax
from jax.sharding import PartitionSpec as P

HEADS = 8


def padded_2(block, sides, width):
    for axis, dim in sides:
        count = lax.axis_size(axis)
        forward = [(i, i + 1) for i in range(count - 1)]
        backward = [(target, source) for source, target in forward]
        low = lax.ppermute(
            lax.slice_in_dim(block, block.shape[dim] - width, None, axis=dim), axis, forward
        )
        high = lax.ppermute(lax.slice_in_dim(block, 0, width, axis=dim), axis, backward)
        block = jnp.concatenate([low, block, high], axis=dim)
    return block


def from_behind(array, axis, by):
    devices = lax.axis_size(axis)
    pairs = [(i, i + by) for i in range(devices) if 0 <= i + by < devices]
    return lax.ppermute(array, axis, pairs)


def conv_space(padded, w_space, height, width):
    channels = padded.shape[-1]
    total = jnp.zeros(padded.shape[:1] + (height, width, channels), jnp.float32)
    for row_off in range(3):
        for col_off in range(3):
            window = padded[:, row_off : row_off + height, col_off : col_off + width, :]
            product = jnp.dot(
                window.reshape(-1, channels),
                w_space[row_off, col_off],
                preferred_element_type=jnp.float32,
            )
            total = total + product.reshape(total.shape)
    return total


def temporal_mix(clip, hidden, earlier, w_time, norm_gain):
    channels = clip.shape[-1]
    frames = hidden.shape[0]
    joined = jnp.concatenate([earlier, hidden], axis=0)
    total = jnp.zeros(hidden.shape, jnp.float32)
    for tap_index in range(3):
        window = joined[2 - tap_index : 2 - tap_index + frames]
        product = jnp.dot(
            window.reshape(-1, channels), w_time[tap_index], preferred_element_type=jnp.float32
        )
        total = total + product.reshape(hidden.shape)
    mixed = (clip.astype(jnp.float32) + total).astype(jnp.bfloat16)
    wide = mixed.astype(jnp.float32)
    scale = lax.rsqrt(jnp.mean(wide * wide, axis=-1, keepdims=True) + 1e-06)
    normed = (wide * scale * norm_gain).astype(jnp.bfloat16)
    return (mixed, normed)


def project(normed, w_qkv):
    channels = normed.shape[-1]
    flattened = jnp.dot(
        normed.reshape(-1, channels), w_qkv, preferred_element_type=jnp.float32
    ).astype(jnp.bfloat16)
    joined = flattened.reshape(normed.shape[:-1] + (3 * channels,))
    return (
        joined[..., :channels],
        joined[..., channels : 2 * channels],
        joined[..., 2 * channels :],
    )


def attend(queries, keyset, valueset, heads):
    frames, rows, cols, channels = queries.shape
    head_dim = channels // heads
    shape = (frames, rows, cols, heads, head_dim)
    scores = jnp.einsum(
        "frwhd,grwhd->rwhfg",
        queries.reshape(shape),
        keyset.reshape(shape),
        preferred_element_type=jnp.float32,
    )
    scores = scores * (1.0 / head_dim**0.5)
    peak = jnp.max(scores, axis=-1, keepdims=True)
    expo = jnp.exp(scores - peak)
    probs = (expo / jnp.sum(expo, axis=-1, keepdims=True)).astype(jnp.bfloat16)
    output = jnp.einsum(
        "rwhfg,grwhd->frwhd", probs, valueset.reshape(shape), preferred_element_type=jnp.float32
    )
    return output.reshape(queries.shape).astype(jnp.bfloat16)


def attend_back(queries, keyset, valueset):
    output = attend(queries, keyset, valueset, HEADS)
    return lax.all_to_all(output, "ta", split_axis=0, concat_axis=2, tiled=True)


def per_device(clip, w_space, w_time, w_qkv, w_out, norm_gain):
    frames, height, width, channels = clip.shape
    rimmed = padded_2(clip, (("gy", 1),), 1)
    padded = jnp.pad(rimmed, ((0, 0), (0, 0), (1, 1), (0, 0)))
    hidden = jax.nn.silu(conv_space(padded, w_space, height, width)).astype(jnp.bfloat16)
    earlier = from_behind(hidden[-2:], "ta", 1)
    mixed, normed = temporal_mix(clip, hidden, earlier, w_time, norm_gain)
    queries, keyset, valueset = project(
        lax.all_to_all(normed, "ta", split_axis=2, concat_axis=0, tiled=True), w_qkv
    )
    attended = attend_back(queries, keyset, valueset)
    projected = jnp.dot(
        attended.reshape(-1, channels), w_out, preferred_element_type=jnp.float32
    ).reshape(clip.shape)
    return (mixed.astype(jnp.float32) + projected).astype(jnp.bfloat16)


def solution(mesh):
    in_specs = (P(("ga", "ta"), "gy", None, None), P(), P(), P(), P(), P())
    out_specs = P(("ga", "ta"), "gy", None, None)
    return jax.shard_map(
        per_device, mesh=mesh, in_specs=in_specs, out_specs=out_specs, check_vma=False
    )
```

profile of v0, /device:TPU:0, one launch (start us, length us, event | category | flops | bytes accessed | tf_op | source)
XLA Modules:
  0.0 112.8 jit_solution(17687621035857392692)
XLA Ops:
  0.0 0.0 copy-start
  0.0 1.2 %fusion.79 = (bf16[4,1,64,512]{3,2,1,0:T(8,128)(2,1)S(1)}, bf16[4,1,64,512]{3,2,1,0:T(8,128)(2,1)S(1)}) fusion(bf16[4,4,64,512]{3,2,1,0:T(8,128)(2,1)} %param.6), kind=kLoop, calls=%fused_computation.87 | loop fusion | bytes 1048576 | tf_op jit(solution)/shard_map/slice | solution.py:15
  1.2 5.0 %collective-permute-start = (bf16[4,1,64,512]{3,2,1,0:T(8,128)(2,1)S(1)}, bf16[4,1,64,512]{3,2,1,0:T(8,128)(2,1)S(1)}, u32[]{:S(2)}, u32[]{:S(2)}) collective-permute-start(bf16[4,1,64,512]{3,2,1,0:T(8,128)(2,1)S(1)} %get-tuple-element.8), channel_id=1, source_target_pairs={{0,1},{1,2},{2,3},{4,5},{5,6},{6,7},{8,9},{9,10},{10,11},{12,13},{... | collective-permute-start | bytes 786440 | tf_op jit(solution)/shard_map/ppermute | solution.py:14
  6.2 0.0 copy-start.2
  6.2 1.4 %collective-permute-start.1 = (bf16[4,1,64,512]{3,2,1,0:T(8,128)(2,1)S(1)}, bf16[4,1,64,512]{3,2,1,0:T(8,128)(2,1)S(1)}, u32[]{:S(2)}, u32[]{:S(2)}) collective-permute-start(bf16[4,1,64,512]{3,2,1,0:T(8,128)(2,1)S(1)} %get-tuple-element.9), channel_id=1, source_target_pairs={{1,0},{2,1},{3,2},{5,4},{6,5},{7,6},{9,8},{10,9},{11,10},{13,12},{... | collective-permute-start | bytes 786440 | tf_op jit(solution)/shard_map/ppermute | solution.py:17
  7.6 0.0 copy-start.4
  7.6 2.2 %fusion.55 = f32[4,4,64,512]{3,2,1,0:T(8,128)S(1)} fusion(bf16[4,4,64,512]{3,2,1,0:T(8,128)(2,1)} %param.6, bf16[3,3,512,512]{3,2,1,0:T(8,128)(2,1)} %param.7), kind=kOutput, calls=%fused_computation.62 | convolution fusion | flops 536870912 | bytes 3670016 | tf_op jit(solution)/shard_map/dot_general | solution.py:34
  9.8 1.9 %collective-permute-done = bf16[4,1,64,512]{3,2,1,0:T(8,128)(2,1)S(1)} collective-permute-done((bf16[4,1,64,512]{3,2,1,0:T(8,128)(2,1)S(1)}, bf16[4,1,64,512]{3,2,1,0:T(8,128)(2,1)S(1)}, u32[]{:S(2)}, u32[]{:S(2)}) %collective-permute-start) | collective-permute-done | bytes 262176 | tf_op jit(solution)/shard_map/ppermute | solution.py:14
  11.7 4.3 %collective-permute-done.1 = bf16[4,1,64,512]{3,2,1,0:T(8,128)(2,1)S(1)} collective-permute-done((bf16[4,1,64,512]{3,2,1,0:T(8,128)(2,1)S(1)}, bf16[4,1,64,512]{3,2,1,0:T(8,128)(2,1)S(1)}, u32[]{:S(2)}, u32[]{:S(2)}) %collective-permute-start.1) | collective-permute-done | bytes 262176 | tf_op jit(solution)/shard_map/ppermute | solution.py:17
  16.0 0.0 copy-done.2
  16.0 0.9 fusion.22
  16.9 0.0 copy-done.4
  16.9 0.7 fusion.35
  17.6 0.7 fusion.37
  18.3 0.7 fusion.39
  19.0 0.7 fusion.41
  19.8 0.7 fusion.43
  20.5 0.7 fusion.23
  21.2 0.7 fusion.27
  21.9 0.0 copy-start.5
  21.9 1.4 %multiply_convert_fusion = bf16[4,4,64,512]{3,2,1,0:T(8,128)(2,1)S(1)} fusion(f32[4,4,64,512]{3,2,1,0:T(8,128)S(1)} %fusion.27, f32[4,4,64,512]{3,2,1,0:T(8,128)S(1)} %fusion.35, f32[4,4,64,512]{3,2,1,0:T(8,128)S(1)} %fusion.37, f32[4,4,64,512]{3,2,1,0:T(8,128)S(1)} %fusion.55, f32[4,4,64,512]{3,2,1,0:T(8,128)S(1)} %fusion.39, ...), kind=kOutput, calls=%fused_computation.25 | convolution fusion | flops 543686656 | bytes 19398656 | tf_op jit(solution)/shard_map/dot_general | solution.py:34
  23.4 1.3 %collective-permute-start.2 = (bf16[2,4,64,512]{3,2,1,0:T(8,128)(2,1)S(1)}, bf16[2,4,64,512]{3,2,1,0:T(8,128)(2,1)S(1)}, u32[]{:S(2)}, u32[]{:S(2)}) collective-permute-start(bf16[2,4,64,512]{3,2,1,0:T(8,128)(2,1)S(1)} %slice.124), channel_id=1, source_target_pairs={{0,4},{4,8},{8,12},{1,5},{5,9},{9,13},{2,6},{6,10},{10,14},{3,7},{... | collective-permute-start | bytes 1572872 | tf_op jit(solution)/shard_map/ppermute | solution.py:25
  24.7 0.0 copy-done.5
  24.7 0.7 fusion.49
  25.4 0.8 collective-permute-done.2
  26.2 0.7 fusion.45
  26.9 0.0 copy-start.6
  26.9 1.0 fusion.5
  27.9 0.0 copy-done.6
  28.0 0.3 fusion.7
  28.3 0.8 copy.22
  29.1 24.7 %all_to_all.30 = bf16[4,4,64,512]{3,1,0,2:T(4,128)(2,1)S(1)} all-to-all(bf16[4,4,64,512]{3,1,0,2:T(4,128)(2,1)S(1)} %copy.22), channel_id=1, replica_groups=mesh['ga'=2,'ta'=4,'gy'=4] {'ta'}, dimensions={2} | all-to-all | bytes 2097152 | tf_op jit(solution)/shard_map/all_to_all | solution.py:107
  53.8 0.6 copy.23
  54.4 0.1 copy.24
  54.4 0.0 copy-done
  54.5 1.8 %convolution_convert_fusion = bf16[1024,1536]{1,0:T(8,128)(2,1)S(1)} fusion(bf16[1024,512]{1,0:T(8,128)(2,1)S(1)} %bitcast.119, bf16[512,1536]{1,0:T(8,128)(2,1)S(1)} %copy-done), kind=kOutput, calls=%fused_computation.5 | convolution fusion | flops 1612185600 | bytes 5767168 | tf_op jit(solution)/shard_map/dot_general | solution.py:63
  56.3 1.7 %fusion.78 = (bf16[16,4,16,512]{3,2,1,0:T(8,128)(2,1)S(1)}, bf16[16,4,16,512]{3,2,1,0:T(8,128)(2,1)}, bf16[16,4,16,512]{3,2,1,0:T(8,128)(2,1)}) fusion(bf16[16,4,16,1536]{3,2,1,0:T(8,128)(2,1)S(1)} %bitcast.117), kind=kLoop, calls=%fused_computation.86 | loop fusion | bytes 6291456 | tf_op jit(solution)/shard_map/slice | solution.py:70
  57.9 2.1 %reshape.84 = bf16[16,4,16,8,64]{4,3,2,1,0:T(8,128)(2,1)} reshape(bf16[16,4,16,512]{3,2,1,0:T(8,128)(2,1)S(1)} %get-tuple-element.5) | data formatting | bytes 2097152 | tf_op jit(solution)/shard_map/reshape | solution.py:89
  60.0 2.8 %reshape.86 = bf16[16,4,16,8,64]{4,3,2,1,0:T(8,128)(2,1)S(1)} reshape(bf16[16,4,16,512]{3,2,1,0:T(8,128)(2,1)} %get-tuple-element.6) | data formatting | bytes 2097152 | tf_op jit(solution)/shard_map/reshape | solution.py:81
  62.8 3.9 %reshape.85 = bf16[16,4,16,8,64]{4,3,2,1,0:T(8,128)(2,1)} reshape(bf16[16,4,16,512]{3,2,1,0:T(8,128)(2,1)} %get-tuple-element.7) | data formatting | bytes 2097152 | tf_op jit(solution)/shard_map/reshape | solution.py:80
  66.7 4.1 %fusion.11 = f32[4,16,8,16,16]{3,4,2,1,0:T(8,128)S(1)} fusion(bf16[16,4,16,8,64]{4,3,2,1,0:T(8,128)(2,1)S(1)} %reshape.86, bf16[16,4,16,8,64]{4,3,2,1,0:T(8,128)(2,1)} %reshape.85), kind=kOutput, calls=%fused_computation.18 | convolution fusion | flops 16777216 | bytes 2621440 | tf_op jit(solution)/shard_map/frwhd,grwhd->rwhfg/dot_general | solution.py:78
  70.8 0.0 copy-start.3
  70.8 17.7 %fusion.80 = (f32[4,16,8,16]{3,2,1,0:T(8,128)S(1)}, f32[4,16,8,16,16]{3,4,2,1,0:T(8,128)S(1)}) fusion(f32[4,16,8,16,16]{3,4,2,1,0:T(8,128)S(1)} %fusion.11), kind=kOutput, calls=%fused_computation.88 | output fusion | flops 524303 | bytes 1081344 | tf_op jit(solution)/shard_map/sub | solution.py:86
  88.6 0.0 copy-done.3
  88.6 1.7 %convert_bitcast_fusion = bf16[16,4,16,8,64]{4,0,3,2,1:T(8,128)(2,1)S(1)} fusion(f32[4,16,8,16,16]{3,4,2,1,0:T(8,128)S(1)} %get-tuple-element.13, f32[4,16,8,16]{3,2,1,0:T(8,128)S(1)} %get-tuple-element.12, bf16[16,4,16,8,64]{4,3,2,1,0:T(8,128)(2,1)S(1)} %copy-done.3), kind=kOutput, calls=%fused_computation.21 | convolution fusion | flops 17563648 | bytes 2654208 | tf_op jit(solution)/shard_map/rwhfg,grwhd->frwhd/dot_general | solution.py:88
  90.3 0.5 copy.29
  90.9 2.0 %convert_element_type.45 = bf16[16,4,16,512]{3,2,1,0:T(8,128)(2,1)} reshape(bf16[16,4,16,8,64]{4,3,2,1,0:T(8,128)(2,1)S(1)} %copy.29) | data formatting | bytes 2097152 | tf_op jit(solution)/shard_map/convert_element_type | solution.py:91
  92.9 0.0 copy-start.7
  92.9 18.0 %all_to_all.31 = bf16[16,4,16,512]{3,2,1,0:T(8,128)(2,1)S(1)} all-to-all(bf16[16,4,16,512]{3,2,1,0:T(8,128)(2,1)} %convert_element_type.45), channel_id=1, replica_groups=mesh['ga'=2,'ta'=4,'gy'=4] {'ta'}, dimensions={0} | all-to-all | bytes 2097152 | tf_op jit(solution)/shard_map/all_to_all | solution.py:96
  111.0 0.1 copy.30
  111.1 0.0 copy-start.1
  111.1 0.0 copy-done.7
  111.1 1.7 %fusion.8 = bf16[4,4,64,512]{3,2,1,0:T(8,128)(2,1)} fusion(bf16[4,4,64,512]{3,2,1,0:T(8,128)(2,1)S(1)} %get-tuple-element.11, bf16[4,4,64,512]{3,2,1,0:T(8,128)(2,1)S(1)} %bitcast.118, bf16[512,512]{1,0:T(8,128)(2,1)S(1)} %copy-done.7), kind=kOutput, calls=%fused_computation.15 | convolution fusion | flops 538443776 | bytes 3670016 | tf_op jit(solution)/shard_map/dot_general | solution.py:110
  112.7 0.0 copy-done.1
  (2 shorter events, 0.0 us)
Async XLA Ops:
  0.0 54.4 %copy-start = (bf16[512,1536]{1,0:T(8,128)(2,1)S(1)}, bf16[512,1536]{1,0:T(8,128)(2,1)}, u32[]{:S(2)}) copy-start(bf16[512,1536]{1,0:T(8,128)(2,1)} %param.9) | copy-start | bytes 4718596
  1.2 10.5 %collective-permute-start = (bf16[4,1,64,512]{3,2,1,0:T(8,128)(2,1)S(1)}, bf16[4,1,64,512]{3,2,1,0:T(8,128)(2,1)S(1)}, u32[]{:S(2)}, u32[]{:S(2)}) collective-permute-start(bf16[4,1,64,512]{3,2,1,0:T(8,128)(2,1)S(1)} %get-tuple-element.8), channel_id=1, source_target_pairs={{0,1},{1,2},{2,3},{4,5},{5,6},{6,7},{8,9},{9,10},{10,11},{12,13},{... | collective-permute-start | bytes 786440 | tf_op jit(solution)/shard_map/ppermute | solution.py:14
  6.2 9.8 %copy-start.2 = (bf16[4,4,64,512]{3,2,1,0:T(8,128)(2,1)S(1)}, bf16[4,4,64,512]{3,2,1,0:T(8,128)(2,1)}, u32[]{:S(2)}) copy-start(bf16[4,4,64,512]{3,2,1,0:T(8,128)(2,1)} %param.6) | copy-start | bytes 3145732
  6.2 9.8 %collective-permute-start.1 = (bf16[4,1,64,512]{3,2,1,0:T(8,128)(2,1)S(1)}, bf16[4,1,64,512]{3,2,1,0:T(8,128)(2,1)S(1)}, u32[]{:S(2)}, u32[]{:S(2)}) collective-permute-start(bf16[4,1,64,512]{3,2,1,0:T(8,128)(2,1)S(1)} %get-tuple-element.9), channel_id=1, source_target_pairs={{1,0},{2,1},{3,2},{5,4},{6,5},{7,6},{9,8},{10,9},{11,10},{13,12},{... | collective-permute-start | bytes 786440 | tf_op jit(solution)/shard_map/ppermute | solution.py:17
  7.6 9.3 %copy-start.4 = (bf16[3,3,512,512]{3,2,1,0:T(8,128)(2,1)S(1)}, bf16[3,3,512,512]{3,2,1,0:T(8,128)(2,1)}, u32[]{:S(2)}) copy-start(bf16[3,3,512,512]{3,2,1,0:T(8,128)(2,1)} %param.7) | copy-start | bytes 14155780
  21.9 2.8 %copy-start.5 = (bf16[3,512,512]{2,1,0:T(8,128)(2,1)S(1)}, bf16[3,512,512]{2,1,0:T(8,128)(2,1)}, u32[]{:S(2)}) copy-start(bf16[3,512,512]{2,1,0:T(8,128)(2,1)} %param.8) | copy-start | bytes 4718596
  23.4 2.8 %collective-permute-start.2 = (bf16[2,4,64,512]{3,2,1,0:T(8,128)(2,1)S(1)}, bf16[2,4,64,512]{3,2,1,0:T(8,128)(2,1)S(1)}, u32[]{:S(2)}, u32[]{:S(2)}) collective-permute-start(bf16[2,4,64,512]{3,2,1,0:T(8,128)(2,1)S(1)} %slice.124), channel_id=1, source_target_pairs={{0,4},{4,8},{8,12},{1,5},{5,9},{9,13},{2,6},{6,10},{10,14},{3,7},{... | collective-permute-start | bytes 1572872 | tf_op jit(solution)/shard_map/ppermute | solution.py:25
  26.9 1.0 copy-start.6
  70.8 17.7 %copy-start.3 = (bf16[16,4,16,8,64]{4,3,2,1,0:T(8,128)(2,1)S(1)}, bf16[16,4,16,8,64]{4,3,2,1,0:T(8,128)(2,1)}, u32[]{:S(2)}) copy-start(bf16[16,4,16,8,64]{4,3,2,1,0:T(8,128)(2,1)} %reshape.84) | copy-start | bytes 3145732
  92.9 18.2 %copy-start.7 = (bf16[512,512]{1,0:T(8,128)(2,1)S(1)}, bf16[512,512]{1,0:T(8,128)(2,1)}, u32[]{:S(2)}) copy-start(bf16[512,512]{1,0:T(8,128)(2,1)} %param.10) | copy-start | bytes 1572868
  111.1 1.7 %copy-start.1 = (bf16[512,1536]{1,0:T(8,128)(2,1)S(1)}, bf16[512,1536]{1,0:T(8,128)(2,1)}, u32[]{:S(2)}) copy-start(bf16[512,1536]{1,0:T(8,128)(2,1)} %param.9) | copy-start | bytes 4718596
where the time goes:
time: 113 us
  blocking collectives  42.7 us (38%)
  matrix products  20.3 us (18%)
  other arithmetic  19 us (17%)
  local copies, waits for them, and re-layouts  15.9 us (14%)
  starting transfers between devices  7.72 us (7%)
  waiting for transfers between devices  6.9 us (6%)
    all_to_all x1, blocking collectives, per_device(): lax.all_to_all(normed, 'ta', split_axis=2, concat_axis=0, tiled=True)  24.7 us
    all_to_all x1, blocking collectives, attend_back(): return lax.all_to_all(output, 'ta', split_axis=0, concat_axis=2, tiled=True)  18 us
    sub x1, other arithmetic, attend(): expo = jnp.exp(scores - peak)  17.7 us
    dot_general x9, matrix products, conv_space(): jnp.dot(window.reshape(-1, channels), w_space[row_off, col_off], preferre...  8.59 us
    ppermute x1, starting transfers between devices, padded_2(): lax.ppermute(lax.slice_in_dim(block, block.shape[dim] - width, None, axis...  4.97 us
    ppermute x1, waiting for transfers between devices, padded_2(): lax.ppermute(lax.slice_in_dim(block, 0, width, axis=dim), axis, backward)  4.27 us
    dot_general x1, matrix products, attend(): jnp.einsum('frwhd,grwhd->rwhfg', queries.reshape(shape), keyset.reshape(s...  4.11 us
    reshape x1, local copies, waits for them, and re-layouts, attend(): queries.reshape(shape)  3.9 us
  transfers between devices with their start and end apart: 3, of which 3 were waited for; matrix products, arithmetic and copies ran while one was open for 3% of the time, Pallas kernels for 0%

commit v1 on v0

--- a/solution.py
+++ b/solution.py
@@ -4,6 +4,22 @@
 from jax.sharding import PartitionSpec as P
 
 HEADS = 8
+
+
+def pairwise_exchange(x, axis, split, join):
+    ways, here = (lax.axis_size(axis), lax.axis_index(axis))
+    width = x.shape[split] // ways
+    dims = list(x.shape)
+    dims[split] = width
+    height = dims[join]
+    dims[join] = height * ways
+    full = jnp.zeros(dims, x.dtype)
+    for mask in range(ways):
+        part = lax.dynamic_slice_in_dim(x, (here ^ mask) * width, width, axis=split)
+        if mask:
+            part = lax.ppermute(part, axis, [(d, d ^ mask) for d in range(ways)])
+        full = lax.dynamic_update_slice_in_dim(full, part, (here ^ mask) * height, axis=join)
+    return full
 
 
 def padded_2(block, sides, width):
@@ -103,9 +119,7 @@
     hidden = jax.nn.silu(conv_space(padded, w_space, height, width)).astype(jnp.bfloat16)
     earlier = from_behind(hidden[-2:], "ta", 1)
     mixed, normed = temporal_mix(clip, hidden, earlier, w_time, norm_gain)
-    queries, keyset, valueset = project(
-        lax.all_to_all(normed, "ta", split_axis=2, concat_axis=0, tiled=True), w_qkv
-    )
+    queries, keyset, valueset = project(pairwise_exchange(normed, "ta", 2, 0), w_qkv)
     attended = attend_back(queries, keyset, valueset)
     projected = jnp.dot(
         attended.reshape(-1, channels), w_out, preferred_element_type=jnp.float32

time: 113 us -> 101 us (0.89)
  blocking collectives: 42.7 us -> 17.1 us
  other arithmetic: 19 us -> 4.66 us
  waiting for transfers between devices: 6.9 us -> 18.6 us
  starting transfers between devices: 7.72 us -> 16.4 us
  matrix products: 20.3 us -> 25.2 us
  local copies, waits for them, and re-layouts: 15.9 us -> 18.7 us
    all_to_all x1 -> x0, blocking collectives: 24.7 us -> none  [per_device(): lax.all_to_all(normed, 'ta', split_axis=2, concat_axis=0, tiled=True)]
    sub x1, other arithmetic: 17.7 us -> 3.42 us  [attend(): expo = jnp.exp(scores - peak)]
    ppermute x0 -> x3, waiting for transfers between devices: none -> 12.4 us  [pairwise_exchange(): part = lax.ppermute(part, axis, [(d, d ^ mask) for d in range(ways)])]
    ppermute x0 -> x3, starting transfers between devices: none -> 8.73 us  [pairwise_exchange(): part = lax.ppermute(part, axis, [(d, d ^ mask) for d in range(ways)])]
    dot_general x1, matrix products: 1.72 us -> 4.44 us  [attend(): jnp.einsum('rwhfg,grwhd->frwhd', probs, valueset.reshape(shape), preferre...]
    convert_element_type x2, local copies, waits for them, and re-layouts: 2.59 us -> 5.06 us  [attend(): return output.reshape(queries.shape).astype(jnp.bfloat16)]
    dot_general x3, matrix products: 2.4 us -> 3.93 us  [temporal_mix(): jnp.dot(window.reshape(-1, channels), w_time[tap_index], preferred_elemen...]
  transfers between devices with their start and end apart: 3 -> 6, of which waited for: 3 -> 4; matrix products, arithmetic and copies ran while one was open for 3% -> 4% of each run, Pallas kernels for 0% -> 0%
where the time goes in v1:
time: 101 us
  matrix products  25.2 us (25%)
  local copies, waits for them, and re-layouts  18.7 us (19%)
  waiting for transfers between devices  18.6 us (18%)
  blocking collectives  17.1 us (17%)
  starting transfers between devices  16.4 us (16%)
  other arithmetic  4.66 us (5%)
    all_to_all x1, blocking collectives, attend_back(): return lax.all_to_all(output, 'ta', split_axis=0, concat_axis=2, tiled=True)  17.1 us
    ppermute x3, waiting for transfers between devices, pairwise_exchange(): part = lax.ppermute(part, axis, [(d, d ^ mask) for d in range(ways)])  12.4 us
    ppermute x3, starting transfers between devices, pairwise_exchange(): part = lax.ppermute(part, axis, [(d, d ^ mask) for d in range(ways)])  8.73 us
    dot_general x9, matrix products, conv_space(): jnp.dot(window.reshape(-1, channels), w_space[row_off, col_off], preferre...  8.59 us
    convert_element_type x2, local copies, waits for them, and re-layouts, attend(): return output.reshape(queries.shape).astype(jnp.bfloat16)  5.06 us
    ppermute x1, starting transfers between devices, padded_2(): lax.ppermute(lax.slice_in_dim(block, block.shape[dim] - width, None, axis...  4.97 us
    dot_general x1, matrix products, attend(): jnp.einsum('frwhd,grwhd->rwhfg', queries.reshape(shape), keyset.reshape(s...  4.75 us
    dot_general x1, matrix products, attend(): jnp.einsum('rwhfg,grwhd->frwhd', probs, valueset.reshape(shape), preferre...  4.44 us
  transfers between devices with their start and end apart: 6, of which 4 were waited for; matrix products, arithmetic and copies ran while one was open for 4% of the time, Pallas kernels for 0%

profile of v1, /device:TPU:0, one launch (start us, length us, event | category | flops | bytes accessed | tf_op | source)
XLA Modules:
  0.0 101.0 jit_solution(13854898638765052977)
XLA Ops:
  0.0 0.0 copy-start
  0.0 1.2 %fusion.79 = (bf16[4,1,64,512]{3,2,1,0:T(8,128)(2,1)S(1)}, bf16[4,1,64,512]{3,2,1,0:T(8,128)(2,1)S(1)}) fusion(bf16[4,4,64,512]{3,2,1,0:T(8,128)(2,1)} %param.6), kind=kLoop, calls=%fused_computation.94 | loop fusion | bytes 1048576 | tf_op jit(solution)/shard_map/slice | solution.py:31
  1.2 5.0 %collective-permute-start = (bf16[4,1,64,512]{3,2,1,0:T(8,128)(2,1)S(1)}, bf16[4,1,64,512]{3,2,1,0:T(8,128)(2,1)S(1)}, u32[]{:S(2)}, u32[]{:S(2)}) collective-permute-start(bf16[4,1,64,512]{3,2,1,0:T(8,128)(2,1)S(1)} %get-tuple-element.12), channel_id=1, source_target_pairs={{0,1},{1,2},{2,3},{4,5},{5,6},{6,7},{8,9},{9,10},{10,11},{12,13},{... | collective-permute-start | bytes 786440 | tf_op jit(solution)/shard_map/ppermute | solution.py:30
  6.2 0.0 copy-start.2
  6.2 1.4 %collective-permute-start.1 = (bf16[4,1,64,512]{3,2,1,0:T(8,128)(2,1)S(1)}, bf16[4,1,64,512]{3,2,1,0:T(8,128)(2,1)S(1)}, u32[]{:S(2)}, u32[]{:S(2)}) collective-permute-start(bf16[4,1,64,512]{3,2,1,0:T(8,128)(2,1)S(1)} %get-tuple-element.13), channel_id=1, source_target_pairs={{1,0},{2,1},{3,2},{5,4},{6,5},{7,6},{9,8},{10,9},{11,10},{13,12},{... | collective-permute-start | bytes 786440 | tf_op jit(solution)/shard_map/ppermute | solution.py:33
  7.6 0.0 copy-start.7
  7.6 2.2 %fusion.55 = f32[4,4,64,512]{3,2,1,0:T(8,128)S(1)} fusion(bf16[4,4,64,512]{3,2,1,0:T(8,128)(2,1)} %param.6, bf16[3,3,512,512]{3,2,1,0:T(8,128)(2,1)} %param.7), kind=kOutput, calls=%fused_computation.62 | convolution fusion | flops 536870912 | bytes 3670016 | tf_op jit(solution)/shard_map/dot_general | solution.py:50
  9.8 1.9 %collective-permute-done = bf16[4,1,64,512]{3,2,1,0:T(8,128)(2,1)S(1)} collective-permute-done((bf16[4,1,64,512]{3,2,1,0:T(8,128)(2,1)S(1)}, bf16[4,1,64,512]{3,2,1,0:T(8,128)(2,1)S(1)}, u32[]{:S(2)}, u32[]{:S(2)}) %collective-permute-start) | collective-permute-done | bytes 262176 | tf_op jit(solution)/shard_map/ppermute | solution.py:30
  11.7 4.3 %collective-permute-done.1 = bf16[4,1,64,512]{3,2,1,0:T(8,128)(2,1)S(1)} collective-permute-done((bf16[4,1,64,512]{3,2,1,0:T(8,128)(2,1)S(1)}, bf16[4,1,64,512]{3,2,1,0:T(8,128)(2,1)S(1)}, u32[]{:S(2)}, u32[]{:S(2)}) %collective-permute-start.1) | collective-permute-done | bytes 262176 | tf_op jit(solution)/shard_map/ppermute | solution.py:33
  16.0 0.0 copy-done.2
  16.0 0.9 fusion.22
  16.9 0.0 copy-done.7
  16.9 0.7 fusion.35
  17.6 0.7 fusion.37
  18.3 0.7 fusion.39
  19.0 0.7 fusion.41
  19.8 0.7 fusion.43
  20.5 0.7 fusion.23
  21.2 0.7 fusion.27
  21.9 1.4 %multiply_convert_fusion = bf16[4,4,64,512]{3,2,1,0:T(8,128)(2,1)S(1)} fusion(f32[4,4,64,512]{3,2,1,0:T(8,128)S(1)} %fusion.27, f32[4,4,64,512]{3,2,1,0:T(8,128)S(1)} %fusion.35, f32[4,4,64,512]{3,2,1,0:T(8,128)S(1)} %fusion.37, f32[4,4,64,512]{3,2,1,0:T(8,128)S(1)} %fusion.55, f32[4,4,64,512]{3,2,1,0:T(8,128)S(1)} %fusion.39, ...), kind=kOutput, calls=%fused_computation.25 | convolution fusion | flops 543686656 | bytes 19398656 | tf_op jit(solution)/shard_map/dot_general | solution.py:50
  23.3 0.0 copy-start.3
  23.4 1.0 copy-done.3
  24.3 0.8 slice.124
  25.2 1.3 %collective-permute-start.2 = (bf16[2,4,64,512]{3,2,1,0:T(8,128)(2,1)}, bf16[2,4,64,512]{3,2,1,0:T(8,128)(2,1)S(1)}, u32[]{:S(2)}, u32[]{:S(2)}) collective-permute-start(bf16[2,4,64,512]{3,2,1,0:T(8,128)(2,1)} %slice.124), channel_id=1, source_target_pairs={{0,4},{4,8},{8,12},{1,5},{5,9},{9,13},{2,6},{6,10},{10,14},{3,7},{... | collective-permute-start | bytes 1572872 | tf_op jit(solution)/shard_map/ppermute | solution.py:41
  26.5 0.0 copy-start.4
  26.5 0.0 copy-start.8
  26.5 2.2 %fusion.49 = f32[4,4,64,512]{3,2,1,0:T(8,128)S(1)} fusion(bf16[4,4,64,512]{3,2,1,0:T(8,128)(2,1)} %copy-done.3, bf16[3,512,512]{2,1,0:T(8,128)(2,1)} %param.8), kind=kOutput, calls=%fused_computation.56 | convolution fusion | flops 536870912 | bytes 3670016 | tf_op jit(solution)/shard_map/dot_general | solution.py:66
  28.7 0.0 collective-permute-done.2
  28.7 0.0 copy-done.4
  28.8 0.0 copy-done.8
  28.8 0.7 fusion.45
  29.5 0.0 copy-start.9
  29.5 1.0 %fusion.5 = (f32[4,4,64]{2,1,0:T(4,128)S(1)}, bf16[4,4,64,512]{3,2,1,0:T(8,128)(2,1)S(1)}) fusion(bf16[3,512,512]{2,1,0:T(8,128)(2,1)S(1)} %copy-done.8, bf16[4,4,64,512]{3,2,1,0:T(8,128)(2,1)S(1)} %copy-done.4, bf16[2,4,64,512]{3,2,1,0:T(8,128)(2,1)S(1)} %collective-permute-done.2, f32[4,4,64,512]{3,2,1,0:T(8,128)S(1)} %fusion.49, ...), kind=kOutput, calls=%fused_computation.12 | convolution fusion | flops 544209920 | bytes 8392704 | tf_op jit(solution)/shard_map/dot_general | solution.py:66
  30.5 0.0 copy-start.5
  30.5 0.0 copy-done.9
  30.5 0.3 fusion.7
  30.9 0.1 broadcast_in_dim.2
  31.0 0.9 constant_dynamic-slice_fusion
  31.9 0.0 copy-done.5
  31.9 6.4 %collective-permute-start.3 = (bf16[4,4,16,512]{3,2,1,0:T(8,128)(2,1)}, bf16[4,4,16,512]{3,2,1,0:T(8,128)(2,1)S(1)}, u32[]{:S(2)}, u32[]{:S(2)}) collective-permute-start(bf16[4,4,16,512]{3,2,1,0:T(8,128)(2,1)} %get-tuple-element.10), channel_id=1, source_target_pairs={{0,4},{4,0},{8,12},{12,8},{1,5},{5,1},{9,13},{13,9},{2,6},{6,2},{1... | collective-permute-start | bytes 786440 | tf_op jit(solution)/shard_map/ppermute | solution.py:20
  38.3 2.3 %collective-permute-start.4 = (bf16[4,4,16,512]{3,2,1,0:T(8,128)(2,1)}, bf16[4,4,16,512]{3,2,1,0:T(8,128)(2,1)S(1)}, u32[]{:S(2)}, u32[]{:S(2)}) collective-permute-start(bf16[4,4,16,512]{3,2,1,0:T(8,128)(2,1)} %get-tuple-element.9), channel_id=1, source_target_pairs={{0,8},{4,12},{8,0},{12,4},{1,9},{5,13},{9,1},{13,5},{2,10},{6,14},... | collective-permute-start | bytes 786440 | tf_op jit(solution)/shard_map/ppermute | solution.py:20
  40.5 0.1 collective-permute-start.5
  40.6 0.0 collective-permute-done.3
  40.7 7.2 %collective-permute-done.4 = bf16[4,4,16,512]{3,2,1,0:T(8,128)(2,1)S(1)} collective-permute-done((bf16[4,4,16,512]{3,2,1,0:T(8,128)(2,1)}, bf16[4,4,16,512]{3,2,1,0:T(8,128)(2,1)S(1)}, u32[]{:S(2)}, u32[]{:S(2)}) %collective-permute-start.4) | collective-permute-done | bytes 262176 | tf_op jit(solution)/shard_map/ppermute | solution.py:20
  47.9 5.2 %collective-permute-done.5 = bf16[4,4,16,512]{3,2,1,0:T(8,128)(2,1)S(1)} collective-permute-done((bf16[4,4,16,512]{3,2,1,0:T(8,128)(2,1)}, bf16[4,4,16,512]{3,2,1,0:T(8,128)(2,1)S(1)}, u32[]{:S(2)}, u32[]{:S(2)}) %collective-permute-start.5) | collective-permute-done | bytes 262176 | tf_op jit(solution)/shard_map/ppermute | solution.py:20
  53.2 0.0 copy-done
  53.2 1.8 %convolution_convert_fusion = bf16[1024,1536]{1,0:T(8,128)(2,1)S(1)} fusion(bf16[1024,512]{1,0:T(8,128)(2,1)S(1)} %bitcast.114, bf16[512,1536]{1,0:T(8,128)(2,1)S(1)} %copy-done), kind=kOutput, calls=%fused_computation.5 | convolution fusion | flops 1612185600 | bytes 5767168 | tf_op jit(solution)/shard_map/dot_general | solution.py:79
  55.0 1.3 %fusion.78 = (bf16[16,4,16,512]{3,2,1,0:T(8,128)(2,1)S(1)}, bf16[16,4,16,512]{3,2,1,0:T(8,128)(2,1)S(1)}, bf16[16,4,16,512]{3,2,1,0:T(8,128)(2,1)}) fusion(bf16[16,4,16,1536]{3,2,1,0:T(8,128)(2,1)S(1)} %bitcast.113), kind=kLoop, calls=%fused_computation.93 | loop fusion | bytes 6291456 | tf_op jit(solution)/shard_map/slice | solution.py:86
  56.3 3.9 %reshape.84 = bf16[16,4,16,8,64]{4,3,2,1,0:T(8,128)(2,1)} reshape(bf16[16,4,16,512]{3,2,1,0:T(8,128)(2,1)} %get-tuple-element.7) | data formatting | bytes 2097152 | tf_op jit(solution)/shard_map/reshape | solution.py:96
  60.2 2.1 %reshape.85 = bf16[16,4,16,8,64]{4,3,2,1,0:T(8,128)(2,1)} reshape(bf16[16,4,16,512]{3,2,1,0:T(8,128)(2,1)S(1)} %get-tuple-element.6) | data formatting | bytes 2097152 | tf_op jit(solution)/shard_map/reshape | solution.py:97
  62.3 4.7 %fusion.11 = f32[4,16,8,16,16]{3,4,2,1,0:T(8,128)S(1)} fusion(bf16[16,4,16,8,64]{4,3,2,1,0:T(8,128)(2,1)} %reshape.85, bf16[16,4,16,8,64]{4,3,2,1,0:T(8,128)(2,1)} %reshape.84), kind=kOutput, calls=%fused_computation.18 | convolution fusion | flops 16777216 | bytes 2621440 | tf_op jit(solution)/shard_map/frwhd,grwhd->rwhfg/dot_general | solution.py:94
  67.0 3.4 %fusion.80 = (f32[4,16,8,16]{3,2,1,0:T(8,128)S(1)}, f32[4,16,8,16,16]{3,4,2,1,0:T(8,128)}) fusion(f32[4,16,8,16,16]{3,4,2,1,0:T(8,128)S(1)} %fusion.11), kind=kOutput, calls=%fused_computation.95 | output fusion | flops 524303 | bytes 1081344 | tf_op jit(solution)/shard_map/sub | solution.py:102
  70.4 2.1 %reshape.83 = bf16[16,4,16,8,64]{4,3,2,1,0:T(8,128)(2,1)} reshape(bf16[16,4,16,512]{3,2,1,0:T(8,128)(2,1)S(1)} %get-tuple-element.5) | data formatting | bytes 2097152 | tf_op jit(solution)/shard_map/reshape | solution.py:105
  72.5 4.4 %convert_bitcast_fusion = bf16[16,4,16,8,64]{4,0,3,2,1:T(8,128)(2,1)S(1)} fusion(f32[4,16,8,16,16]{3,4,2,1,0:T(8,128)} %get-tuple-element.17, f32[4,16,8,16]{3,2,1,0:T(8,128)S(1)} %get-tuple-element.16, bf16[16,4,16,8,64]{4,3,2,1,0:T(8,128)(2,1)} %reshape.83), kind=kOutput, calls=%fused_computation.21 | convolution fusion | flops 17563648 | bytes 2654208 | tf_op jit(solution)/shard_map/rwhfg,grwhd->frwhd/dot_general | solution.py:104
  77.0 1.9 %copy.12 = bf16[16,4,16,8,64]{4,3,2,1,0:T(8,128)(2,1)} copy(bf16[16,4,16,8,64]{4,0,3,2,1:T(8,128)(2,1)S(1)} %convert_bitcast_fusion) | data formatting | bytes 2097152 | tf_op jit(solution)/shard_map/convert_element_type | solution.py:107
  78.8 3.2 %convert_element_type.45 = bf16[16,4,16,512]{3,2,1,0:T(8,128)(2,1)S(1)} reshape(bf16[16,4,16,8,64]{4,3,2,1,0:T(8,128)(2,1)} %copy.12) | data formatting | bytes 2097152 | tf_op jit(solution)/shard_map/convert_element_type | solution.py:107
  82.0 0.0 copy-start.6
  82.0 0.0 copy-start.10
  82.0 17.1 %all_to_all.15 = bf16[16,4,16,512]{3,2,1,0:T(8,128)(2,1)S(1)} all-to-all(bf16[16,4,16,512]{3,2,1,0:T(8,128)(2,1)S(1)} %convert_element_type.45), channel_id=1, replica_groups=mesh['ga'=2,'ta'=4,'gy'=4] {'ta'}, dimensions={0} | all-to-all | bytes 2097152 | tf_op jit(solution)/shard_map/all_to_all | solution.py:112
  99.1 0.1 copy.13
  99.2 0.0 copy-start.1
  99.3 0.0 copy-done.6
  99.3 0.0 copy-done.10
  99.3 1.7 %fusion.8 = bf16[4,4,64,512]{3,2,1,0:T(8,128)(2,1)} fusion(bf16[4,4,64,512]{3,2,1,0:T(8,128)(2,1)S(1)} %copy-done.6, bf16[4,4,64,512]{3,2,1,0:T(8,128)(2,1)S(1)} %bitcast.115, bf16[512,512]{1,0:T(8,128)(2,1)S(1)} %copy-done.10), kind=kOutput, calls=%fused_computation.15 | convolution fusion | flops 538443776 | bytes 3670016 | tf_op jit(solution)/shard_map/dot_general | solution.py:124
  (5 shorter events, 0.1 us)
Async XLA Ops:
  0.0 53.2 %copy-start = (bf16[512,1536]{1,0:T(8,128)(2,1)S(1)}, bf16[512,1536]{1,0:T(8,128)(2,1)}, u32[]{:S(2)}) copy-start(bf16[512,1536]{1,0:T(8,128)(2,1)} %param.9) | copy-start | bytes 4718596
  1.2 10.5 %collective-permute-start = (bf16[4,1,64,512]{3,2,1,0:T(8,128)(2,1)S(1)}, bf16[4,1,64,512]{3,2,1,0:T(8,128)(2,1)S(1)}, u32[]{:S(2)}, u32[]{:S(2)}) collective-permute-start(bf16[4,1,64,512]{3,2,1,0:T(8,128)(2,1)S(1)} %get-tuple-element.12), channel_id=1, source_target_pairs={{0,1},{1,2},{2,3},{4,5},{5,6},{6,7},{8,9},{9,10},{10,11},{12,13},{... | collective-permute-start | bytes 786440 | tf_op jit(solution)/shard_map/ppermute | solution.py:30
  6.2 9.8 %copy-start.2 = (bf16[4,4,64,512]{3,2,1,0:T(8,128)(2,1)S(1)}, bf16[4,4,64,512]{3,2,1,0:T(8,128)(2,1)}, u32[]{:S(2)}) copy-start(bf16[4,4,64,512]{3,2,1,0:T(8,128)(2,1)} %param.6) | copy-start | bytes 3145732
  6.2 9.8 %collective-permute-start.1 = (bf16[4,1,64,512]{3,2,1,0:T(8,128)(2,1)S(1)}, bf16[4,1,64,512]{3,2,1,0:T(8,128)(2,1)S(1)}, u32[]{:S(2)}, u32[]{:S(2)}) collective-permute-start(bf16[4,1,64,512]{3,2,1,0:T(8,128)(2,1)S(1)} %get-tuple-element.13), channel_id=1, source_target_pairs={{1,0},{2,1},{3,2},{5,4},{6,5},{7,6},{9,8},{10,9},{11,10},{13,12},{... | collective-permute-start | bytes 786440 | tf_op jit(solution)/shard_map/ppermute | solution.py:33
  7.6 9.3 %copy-start.7 = (bf16[3,3,512,512]{3,2,1,0:T(8,128)(2,1)S(1)}, bf16[3,3,512,512]{3,2,1,0:T(8,128)(2,1)}, u32[]{:S(2)}) copy-start(bf16[3,3,512,512]{3,2,1,0:T(8,128)(2,1)} %param.7) | copy-start | bytes 14155780
  23.3 1.0 copy-start.3
  25.2 3.6 %collective-permute-start.2 = (bf16[2,4,64,512]{3,2,1,0:T(8,128)(2,1)}, bf16[2,4,64,512]{3,2,1,0:T(8,128)(2,1)S(1)}, u32[]{:S(2)}, u32[]{:S(2)}) collective-permute-start(bf16[2,4,64,512]{3,2,1,0:T(8,128)(2,1)} %slice.124), channel_id=1, source_target_pairs={{0,4},{4,8},{8,12},{1,5},{5,9},{9,13},{2,6},{6,10},{10,14},{3,7},{... | collective-permute-start | bytes 1572872 | tf_op jit(solution)/shard_map/ppermute | solution.py:41
  26.5 2.2 %copy-start.4 = (bf16[4,4,64,512]{3,2,1,0:T(8,128)(2,1)S(1)}, bf16[4,4,64,512]{3,2,1,0:T(8,128)(2,1)}, u32[]{:S(2)}) copy-start(bf16[4,4,64,512]{3,2,1,0:T(8,128)(2,1)} %copy-done.3) | copy-start | bytes 3145732
  26.5 2.2 %copy-start.8 = (bf16[3,512,512]{2,1,0:T(8,128)(2,1)S(1)}, bf16[3,512,512]{2,1,0:T(8,128)(2,1)}, u32[]{:S(2)}) copy-start(bf16[3,512,512]{2,1,0:T(8,128)(2,1)} %param.8) | copy-start | bytes 4718596
  29.5 1.1 %copy-start.9 = (f32[512]{0:T(512)S(1)}, f32[512]{0:T(512)}, u32[]{:S(2)}) copy-start(f32[512]{0:T(512)} %param.11) | copy-start | bytes 6148
  30.5 1.4 %copy-start.5 = (bf16[4,4,64,512]{3,2,1,0:T(8,128)(2,1)}, bf16[4,4,64,512]{3,2,1,0:T(8,128)(2,1)S(1)}, u32[]{:S(2)}) copy-start(bf16[4,4,64,512]{3,2,1,0:T(8,128)(2,1)S(1)} %get-tuple-element.15) | copy-start | bytes 3145732
  31.9 8.7 %collective-permute-start.3 = (bf16[4,4,16,512]{3,2,1,0:T(8,128)(2,1)}, bf16[4,4,16,512]{3,2,1,0:T(8,128)(2,1)S(1)}, u32[]{:S(2)}, u32[]{:S(2)}) collective-permute-start(bf16[4,4,16,512]{3,2,1,0:T(8,128)(2,1)} %get-tuple-element.10), channel_id=1, source_target_pairs={{0,4},{4,0},{8,12},{12,8},{1,5},{5,1},{9,13},{13,9},{2,6},{6,2},{1... | collective-permute-start | bytes 786440 | tf_op jit(solution)/shard_map/ppermute | solution.py:20
  38.3 9.6 %collective-permute-start.4 = (bf16[4,4,16,512]{3,2,1,0:T(8,128)(2,1)}, bf16[4,4,16,512]{3,2,1,0:T(8,128)(2,1)S(1)}, u32[]{:S(2)}, u32[]{:S(2)}) collective-permute-start(bf16[4,4,16,512]{3,2,1,0:T(8,128)(2,1)} %get-tuple-element.9), channel_id=1, source_target_pairs={{0,8},{4,12},{8,0},{12,4},{1,9},{5,13},{9,1},{13,5},{2,10},{6,14},... | collective-permute-start | bytes 786440 | tf_op jit(solution)/shard_map/ppermute | solution.py:20
  40.5 12.6 %collective-permute-start.5 = (bf16[4,4,16,512]{3,2,1,0:T(8,128)(2,1)}, bf16[4,4,16,512]{3,2,1,0:T(8,128)(2,1)S(1)}, u32[]{:S(2)}, u32[]{:S(2)}) collective-permute-start(bf16[4,4,16,512]{3,2,1,0:T(8,128)(2,1)} %get-tuple-element.8), channel_id=1, source_target_pairs={{0,12},{4,8},{8,4},{12,0},{1,13},{5,9},{9,5},{13,1},{2,14},{6,10},... | collective-permute-start | bytes 786440 | tf_op jit(solution)/shard_map/ppermute | solution.py:20
  82.0 17.2 %copy-start.6 = (bf16[4,4,64,512]{3,2,1,0:T(8,128)(2,1)S(1)}, bf16[4,4,64,512]{3,2,1,0:T(8,128)(2,1)}, u32[]{:S(2)}) copy-start(bf16[4,4,64,512]{3,2,1,0:T(8,128)(2,1)} %copy-done.5) | copy-start | bytes 3145732
  82.0 17.2 %copy-start.10 = (bf16[512,512]{1,0:T(8,128)(2,1)S(1)}, bf16[512,512]{1,0:T(8,128)(2,1)}, u32[]{:S(2)}) copy-start(bf16[512,512]{1,0:T(8,128)(2,1)} %param.10) | copy-start | bytes 1572868
  99.2 1.7 %copy-start.1 = (bf16[512,1536]{1,0:T(8,128)(2,1)S(1)}, bf16[512,1536]{1,0:T(8,128)(2,1)}, u32[]{:S(2)}) copy-start(bf16[512,1536]{1,0:T(8,128)(2,1)} %param.9) | copy-start | bytes 4718596
